TPU v7x, 128 devices: a whole 4x4x4 slice. The times are simulated.
128 devices in a mesh: grp: 16 (over z, x), ep: 8 (over y, core).
Axes of the slice: x: 4, y: 4, z: 4, core: 2. Of those that a mesh axis runs over, the one named last changes fastest.
Arguments:
- tokens: bfloat16 [256, 7168], P(('grp', 'ep')), may hold values from -6 to 6
- expert_ids: int32 [256, 8], P(('grp', 'ep')), may hold values from 0 to 15, all different within a row; in each aligned block of 2 rows (0 to 1, 2 to 3, ...) at most 2 rows name the same one
- gate_ints: int32 [256, 8], P(('grp', 'ep')), may hold values from 1 to 16
- w_gate: bfloat16 [16, 7168, 2048], P('grp', None, 'ep'), may hold values from -0.0625 to 0.0625
- w_up: bfloat16 [16, 7168, 2048], P('grp', None, 'ep'), may hold values from -0.0625 to 0.0625
- w_down: bfloat16 [16, 2048, 7168], P('grp', 'ep'), may hold values from -0.125 to 0.125
Outputs:
- mixed: bfloat16 [256, 7168], P(('grp', 'ep'))
Inputs may be any that keep to these rules, and one draw needn't show every extreme that they name: `expert_ids`: each row names 8 different experts. Within the 2 rows of one device no expert is named more than 2 times, a bound that some block reaches on some device in every draw.
All inputs are finite; a program needn't handle non-finite values.
Results may differ from a plain program's by a relative error of at most 0.015.
Values may be sent and summed in bfloat16 or wider, within the bound.
No kernel may reach another device: no remote copies, remote signals or barrier semaphores. Data moves between devices by JAX's collectives and lax.ppermute only.
A program may use at most 64 MiB of HBM per device.

v0:
```python
import jax
import jax.numpy as jnp
from jax import lax
from jax.sharding import PartitionSpec as P


def local(tokens, expert_ids, gate_ints, w_gate, w_up, w_down):
    groups = lax.axis_size("grp")
    tok_rows, width = tokens.shape
    picks = expert_ids.shape[1]
    capacity = min(tok_rows, max(2, 3 * tok_rows * picks // (2 * groups)))
    routes = expert_ids.reshape(-1)
    onehot = (routes[:, None] == jnp.arange(groups, dtype=jnp.int32)[None, :]).astype(jnp.int32)
    earlier = jnp.cumsum(onehot, axis=0) - onehot
    slots = jnp.sum(earlier * onehot, axis=1)
    position = routes * capacity + slots
    token_index = jnp.arange(tok_rows * picks, dtype=jnp.int32) // picks
    table = jnp.zeros((groups * capacity,), jnp.int32).at[position].set(token_index)
    filled = jnp.zeros((groups * capacity,), jnp.bfloat16).at[position].set(1.0)
    dispatch = (tokens[table] * filled[:, None]).reshape(groups, capacity, width)
    gate_w = w_gate[0]
    up_w = w_up[0]
    down_w = w_down[0]
    arrived = lax.all_to_all(dispatch, "grp", split_axis=0, concat_axis=0, tiled=True)
    arrived = arrived.reshape(groups * capacity, width)
    rows = lax.all_gather(arrived, "ep", axis=0, tiled=True)
    gate = jnp.dot(rows, gate_w, preferred_element_type=jnp.float32)
    up = jnp.dot(rows, up_w, preferred_element_type=jnp.float32)
    hidden = (jax.nn.silu(gate) * up).astype(jnp.bfloat16)
    summed = lax.psum_scatter(
        jnp.dot(hidden, down_w, preferred_element_type=jnp.float32).astype(jnp.bfloat16),
        "ep",
        scatter_dimension=0,
        tiled=True,
    ).astype(jnp.float32)
    summed = summed.astype(jnp.bfloat16).reshape(groups, capacity, width)
    expert_out = lax.all_to_all(summed, "grp", split_axis=0, concat_axis=0, tiled=True)
    flat_out = expert_out.reshape(groups * capacity, width)
    picked = flat_out[position].astype(jnp.float32)
    scores = gate_ints.astype(jnp.float32)
    weight = scores / jnp.sum(scores, axis=1, keepdims=True)
    mixed = jnp.sum(picked.reshape(tok_rows, picks, width) * weight[:, :, None], axis=1)
    return mixed.astype(jnp.bfloat16)


def solution(mesh):
    in_specs = (
        P(("grp", "ep"), None),
        P(("grp", "ep"), None),
        P(("grp", "ep"), None),
        P("grp", None, "ep"),
        P("grp", None, "ep"),
        P("grp", "ep", None),
    )
    out_specs = P(("grp", "ep"), None)
    return jax.shard_map(local, mesh=mesh, in_specs=in_specs, out_specs=out_specs, check_vma=False)
```

profile of v0, /device:TPU:0, one launch (start us, length us, event | category | flops | bytes accessed | tf_op | source)
XLA Modules:
  0.0 137.2 jit_solution(14040806807213435363)
XLA Ops:
  6.5 0.0 copy-start
  6.5 0.0 all-gather.2.cloned.1.call-start
  6.5 0.8 eq.15
  7.3 0.7 broadcast_multiply_fusion.1
  8.0 0.1 fusion.20
  8.1 0.2 select_reduce_fusion
  8.3 0.1 mul.43
  8.4 0.6 scatter_custom_fusion
  9.0 0.0 copy-done
  9.0 0.8 gather_fusion
  9.9 0.2 gather.9
  10.1 0.7 scatter_custom_fusion.1
  10.7 0.1 mul.45
  10.8 0.5 broadcast_multiply_fusion
  11.3 18.6 %all_to_all.10 = bf16[16,2,7168]{2,1,0:T(2,128)(2,1)S(1)} all-to-all(bf16[16,2,7168]{2,1,0:T(2,128)(2,1)S(1)} %broadcast_multiply_fusion), channel_id=1, replica_groups=mesh['grp'=16,'ep'=8] {'grp'}, dimensions={0} | all-to-all | bytes 917504 | tf_op jit(solution)/shard_map/all_to_all | solution.py:24
  29.9 0.9 reshape.53
  30.8 0.0 all-gather.2.cloned.1.call-update
  30.9 0.0 reduce-scatter.2.cloned.1.call-start
  30.9 27.6 %all-gather.2.cloned.1.call-done = bf16[256,7168]{1,0:T(8,128)(2,1)} async-done(((bf16[32,7168]{1,0:T(8,128)(2,1)}), bf16[256,7168]{1,0:T(8,128)(2,1)}) %all-gather.2.cloned.1.call-update) | async-done | bytes 3670032 | tf_op jit(solution)/shard_map/all_gather | solution.py:26
  58.5 4.3 %fusion.3 = f32[256,256]{1,0:T(8,128)S(1)} fusion(bf16[256,7168]{1,0:T(8,128)(2,1)} %all-gather.2.cloned.1.call-done, bf16[1,7168,256]{2,1,0:T(8,128)(2,1)} %param.9), kind=kOutput, calls=%fused_computation.8 | convolution fusion | flops 939524096 | bytes 7602176 | tf_op jit(solution)/shard_map/dot_general | solution.py:27
  62.8 10.0 %convolution_convert_fusion = bf16[256,7168]{1,0:T(8,128)(2,1)} fusion(bf16[1,256,7168]{2,1,0:T(8,128)(2,1)} %param.11, bf16[256,7168]{1,0:T(8,128)(2,1)} %all-gather.2.cloned.1.call-done, bf16[1,7168,256]{2,1,0:T(8,128)(2,1)} %param.10, f32[256,256]{1,0:T(8,128)S(1)} %fusion.3), kind=kOutput, calls=%fused_computation.4 | convolution fusion | flops 1881276416 | bytes 14942208 | tf_op jit(solution)/shard_map/dot_general | solution.py:31
  72.9 0.0 copy-start.1
  72.9 0.0 reduce-scatter.2.cloned.1.call-update
  72.9 37.0 %reduce-scatter.2.cloned.1.call-done = bf16[32,7168]{1,0:T(8,128)(2,1)} async-done(((bf16[256,7168]{1,0:T(8,128)(2,1)}), bf16[32,7168]{1,0:T(8,128)(2,1)}) %reduce-scatter.2.cloned.1.call-update) | async-done | bytes 458768 | tf_op jit(solution)/shard_map/reduce_scatter | solution.py:30
  109.9 2.0 %reshape.54 = bf16[16,2,7168]{2,1,0:T(2,128)(2,1)} reshape(bf16[32,7168]{1,0:T(8,128)(2,1)} %reduce-scatter.2.cloned.1.call-done) | data formatting | bytes 917504 | tf_op jit(solution)/shard_map/reshape | solution.py:36
  111.9 6.9 %all-to-all-start.1 = ((bf16[16,2,7168]{2,1,0:T(2,128)(2,1)}), bf16[16,2,7168]{2,1,0:T(2,128)(2,1)S(1)}, u32[]{:S(2)}, u32[]{:S(2)}) async-start(bf16[16,2,7168]{2,1,0:T(2,128)(2,1)} %reshape.54), calls=%async_computation.2 | async-start | bytes 917504 | tf_op jit(solution)/shard_map/all_to_all | solution.py:37
  118.8 0.0 copy-done.1
  118.8 0.1 convert_reduce_fusion
  119.0 0.1 convert_divide_fusion
  119.0 9.5 %all-to-all-done.1 = bf16[16,2,7168]{2,1,0:T(2,128)(2,1)S(1)} async-done(((bf16[16,2,7168]{2,1,0:T(2,128)(2,1)}), bf16[16,2,7168]{2,1,0:T(2,128)(2,1)S(1)}, u32[]{:S(2)}, u32[]{:S(2)}) %all-to-all-start.1) | async-done | bytes 458784 | tf_op jit(solution)/shard_map/all_to_all | solution.py:37
  128.6 0.2 reshape.55
  128.8 0.7 gather_fusion.1
  129.4 0.9 fusion.13
  (7 shorter events, 0.1 us)
Async XLA Ops:
  6.5 2.5 %copy-start = (bf16[2,7168]{1,0:T(2,128)(2,1)S(1)}, bf16[2,7168]{1,0:T(2,128)(2,1)}, u32[]{:S(2)}) copy-start(bf16[2,7168]{1,0:T(2,128)(2,1)} %param.6) | copy-start | bytes 86020
  6.5 52.0 %all-gather.2.cloned.1.call-start = ((), (), s32[]{:S(2)}) async-start(), calls=%async_computation.3 | async-start | bytes 4128768 | tf_op jit(solution)/shard_map/all_gather | solution.py:26
  30.9 79.1 %reduce-scatter.2.cloned.1.call-start = ((), (), s32[]{:S(2)}) async-start(), calls=%async_computation.4 | async-start | bytes 4128768 | tf_op jit(solution)/shard_map/reduce_scatter | solution.py:30
  72.9 46.0 %copy-start.1 = (s32[2,8]{1,0:T(2,128)S(1)}, s32[2,8]{1,0:T(2,128)}, u32[]{:S(2)}) copy-start(s32[2,8]{1,0:T(2,128)} %param.8) | copy-start | bytes 196
  111.9 16.7 %all-to-all-start.1 = ((bf16[16,2,7168]{2,1,0:T(2,128)(2,1)}), bf16[16,2,7168]{2,1,0:T(2,128)(2,1)S(1)}, u32[]{:S(2)}, u32[]{:S(2)}) async-start(bf16[16,2,7168]{2,1,0:T(2,128)(2,1)} %reshape.54), calls=%async_computation.2 | async-start | bytes 917504 | tf_op jit(solution)/shard_map/all_to_all | solution.py:37
Sparse Core Ops, SparseCore 0:
  31.0 27.5 all-gather.1
  73.0 36.8 reduce-scatter.1
where the time goes:
time: 138 us; the launch traced here: 137 us
  waiting for transfers between devices  74.2 us (54%)
  blocking collectives  18.6 us (13%)
  matrix products  14.3 us (10%)
  between operations  13.5 us (10%)
  local copies, waits for them, and re-layouts  7 us (5%)
  starting transfers between devices  6.99 us (5%)
  other arithmetic  2.53 us (2%)
    reduce_scatter x1, waiting for transfers between devices, local(): lax.psum_scatter(jnp.dot(hidden, down_w, preferred_element_type=jnp.float...  37 us
    all_gather x1, waiting for transfers between devices, local(): rows = lax.all_gather(arrived, 'ep', axis=0, tiled=True)  27.6 us
    all_to_all x1, blocking collectives, local(): lax.all_to_all(dispatch, 'grp', split_axis=0, concat_axis=0, tiled=True)  18.6 us
    dot_general x1, matrix products, local(): jnp.dot(hidden, down_w, preferred_element_type=jnp.float32)  10 us
    all_to_all x1, waiting for transfers between devices, local(): lax.all_to_all(summed, 'grp', split_axis=0, concat_axis=0, tiled=True)  9.54 us
    all_to_all x1, starting transfers between devices, local(): lax.all_to_all(summed, 'grp', split_axis=0, concat_axis=0, tiled=True)  6.95 us
    dot_general x1, matrix products, local(): gate = jnp.dot(rows, gate_w, preferred_element_type=jnp.float32)  4.26 us
  transfers between devices with their start and end apart: 3, of which 3 were waited for; matrix products, arithmetic and copies ran while one was open for 0% of the time, Pallas kernels for 0%

commit v1 on v0

--- a/solution.py
+++ b/solution.py
@@ -2,6 +2,12 @@
 import jax.numpy as jnp
 from jax import lax
 from jax.sharding import PartitionSpec as P
+
+
+def map_state(x0, axis_no):
+    a_next = list(x0.shape[1:])
+    a_next[axis_no] *= x0.shape[0]
+    return jnp.moveaxis(x0, 0, axis_no).reshape(a_next)
 
 
 def local(tokens, expert_ids, gate_ints, w_gate, w_up, w_down):
@@ -23,7 +29,27 @@
     down_w = w_down[0]
     arrived = lax.all_to_all(dispatch, "grp", split_axis=0, concat_axis=0, tiled=True)
     arrived = arrived.reshape(groups * capacity, width)
-    rows = lax.all_gather(arrived, "ep", axis=0, tiled=True)
+    nodes = []
+    fan = jax.lax.axis_size("ep")
+    for dev in range(fan):
+        nodes.append((dev, (dev + 1) % fan))
+    pieces_in = []
+    for c, k0 in nodes:
+        pieces_in.append((k0, c))
+    far_arr, passed = ([], [])
+    for dev_j in range(fan - 1):
+        if dev_j % 2 == 0:
+            far_arr.append(
+                jax.lax.ppermute(far_arr[-1] if far_arr else arrived, axis_name="ep", perm=nodes)
+            )
+        else:
+            passed.append(
+                jax.lax.ppermute(passed[-1] if passed else arrived, axis_name="ep", perm=pieces_in)
+            )
+    placed = jnp.stack([*far_arr[::-1], arrived, *passed])
+    y1 = jax.lax.axis_index("ep") - len(far_arr)
+    placed = placed[(jnp.arange(fan) - y1) % fan]
+    rows = map_state(placed, 0)
     gate = jnp.dot(rows, gate_w, preferred_element_type=jnp.float32)
     up = jnp.dot(rows, up_w, preferred_element_type=jnp.float32)
     hidden = (jax.nn.silu(gate) * up).astype(jnp.bfloat16)

time: 138 us -> 153 us (1.11)
  local copies, waits for them, and re-layouts: 7 us -> 18.5 us
  starting transfers between devices: 6.99 us -> 15.9 us
  waiting for transfers between devices: 74.2 us -> 69.2 us
    all_gather x1 -> x0, waiting for transfers between devices: 27.6 us -> none  [local(): rows = lax.all_gather(arrived, 'ep', axis=0, tiled=True)]
    ppermute x0 -> x7, waiting for transfers between devices: none -> 27.5 us  [the longest x4 27.4 us: local(): jax.lax.ppermute(far_arr[-1] if far_arr else arrived, axis_name='ep', per...]
    ppermute x0 -> x7, starting transfers between devices: none -> 8.9 us  [the longest x3 8.87 us: local(): jax.lax.ppermute(passed[-1] if passed else arrived, axis_name='ep', perm=...]
    unnamed x4 -> x11, local copies, waits for them, and re-layouts: 0.01 us -> 6.7 us
    reduce_scatter x1, waiting for transfers between devices: 37 us -> 32.1 us  [local(): lax.psum_scatter(jnp.dot(hidden, down_w, preferred_element_type=jnp.float...]
    gather x0 -> x1, local copies, waits for them, and re-layouts: none -> 4.65 us  [local(): placed = placed[(jnp.arange(fan) - y1) % fan]]
  transfers between devices with their start and end apart: 3 -> 9, of which waited for: 3 -> 6; matrix products, arithmetic and copies ran while one was open for 0% -> 5% of each run, Pallas kernels for 0% -> 0%
where the time goes in v1:
time: 153 us; the launch traced here: 152 us
  waiting for transfers between devices  69.2 us (45%)
  blocking collectives  18.6 us (12%)
  local copies, waits for them, and re-layouts  18.5 us (12%)
  starting transfers between devices  15.9 us (10%)
  matrix products  14.3 us (9%)
  between operations  13.5 us (9%)
  other arithmetic  2.55 us (2%)
    reduce_scatter x1, waiting for transfers between devices, local(): lax.psum_scatter(jnp.dot(hidden, down_w, preferred_element_type=jnp.float...  32.1 us
    ppermute x4, waiting for transfers between devices, local(): jax.lax.ppermute(far_arr[-1] if far_arr else arrived, axis_name='ep', per...  27.4 us
    all_to_all x1, blocking collectives, local(): lax.all_to_all(dispatch, 'grp', split_axis=0, concat_axis=0, tiled=True)  18.6 us
    dot_general x1, matrix products, local(): jnp.dot(hidden, down_w, preferred_element_type=jnp.float32)  10 us
    all_to_all x1, waiting for transfers between devices, local(): lax.all_to_all(summed, 'grp', split_axis=0, concat_axis=0, tiled=True)  9.54 us
    ppermute x3, starting transfers between devices, local(): jax.lax.ppermute(passed[-1] if passed else arrived, axis_name='ep', perm=...  8.87 us
    all_to_all x1, starting transfers between devices, local(): lax.all_to_all(summed, 'grp', split_axis=0, concat_axis=0, tiled=True)  6.96 us
    unnamed x11, local copies, waits for them, and re-layouts  6.7 us
  transfers between devices with their start and end apart: 9, of which 6 were waited for; matrix products, arithmetic and copies ran while one was open for 5% of the time, Pallas kernels for 0%

profile of v1, /device:TPU:0, one launch (start us, length us, event | category | flops | bytes accessed | tf_op | source)
XLA Modules:
  0.0 152.5 jit_solution(3803819207867826928)
XLA Ops:
  6.5 0.0 copy-start
  6.5 0.0 reduce-scatter.2.cloned.1.call-start
  6.5 0.8 eq.17
  7.3 0.7 broadcast_multiply_fusion.1
  8.0 0.1 fusion.20
  8.1 0.2 select_reduce_fusion
  8.3 0.1 mul.43
  8.4 0.6 scatter_custom_fusion
  9.0 0.0 copy-done
  9.0 0.8 gather_fusion
  9.9 0.2 gather.12
  10.1 0.7 scatter_custom_fusion.1
  10.7 0.1 mul.45
  10.8 0.5 broadcast_multiply_fusion
  11.3 18.6 %all_to_all.10 = bf16[16,2,7168]{2,1,0:T(2,128)(2,1)S(1)} all-to-all(bf16[16,2,7168]{2,1,0:T(2,128)(2,1)S(1)} %broadcast_multiply_fusion), channel_id=1, replica_groups=mesh['grp'=16,'ep'=8] {'grp'}, dimensions={0} | all-to-all | bytes 917504 | tf_op jit(solution)/shard_map/all_to_all | solution.py:30
  29.9 0.2 reshape.105
  30.1 0.0 collective-permute-start
  30.1 9.1 %collective-permute-done = bf16[32,7168]{1,0:T(8,128)(2,1)S(1)} collective-permute-done((bf16[32,7168]{1,0:T(8,128)(2,1)S(1)}, bf16[32,7168]{1,0:T(8,128)(2,1)S(1)}, u32[]{:S(2)}, u32[]{:S(2)}) %collective-permute-start) | collective-permute-done | bytes 458784 | tf_op jit(solution)/shard_map/ppermute | solution.py:43
  39.2 0.0 collective-permute-start.1
  39.2 3.0 %collective-permute-start.4 = (bf16[32,7168]{1,0:T(8,128)(2,1)S(1)}, bf16[32,7168]{1,0:T(8,128)(2,1)S(1)}, u32[]{:S(2)}, u32[]{:S(2)}) collective-permute-start(bf16[32,7168]{1,0:T(8,128)(2,1)S(1)} %reshape.105), channel_id=1, source_target_pairs={{1,0},{2,1},{3,2},{4,3},{5,4},{6,5},{7,6},{0,7},{9,8},{10,9},{11,1... | collective-permute-start | bytes 1376264 | tf_op jit(solution)/shard_map/ppermute | solution.py:47
  42.1 6.2 %collective-permute-done.1 = bf16[32,7168]{1,0:T(8,128)(2,1)S(1)} collective-permute-done((bf16[32,7168]{1,0:T(8,128)(2,1)S(1)}, bf16[32,7168]{1,0:T(8,128)(2,1)S(1)}, u32[]{:S(2)}, u32[]{:S(2)}) %collective-permute-start.1) | collective-permute-done | bytes 458784 | tf_op jit(solution)/shard_map/ppermute | solution.py:43
  48.3 0.0 collective-permute-start.2
  48.3 0.0 collective-permute-done.4
  48.3 3.0 %collective-permute-start.5 = (bf16[32,7168]{1,0:T(8,128)(2,1)S(1)}, bf16[32,7168]{1,0:T(8,128)(2,1)S(1)}, u32[]{:S(2)}, u32[]{:S(2)}) collective-permute-start(bf16[32,7168]{1,0:T(8,128)(2,1)S(1)} %collective-permute-done.4), channel_id=1, source_target_pairs={{1,0},{2,1},{3,2},{4,3},{5,4},{6,5},{7,6},{0,7},{9,8},{10,9},{11,1... | collective-permute-start | bytes 1376264 | tf_op jit(solution)/shard_map/ppermute | solution.py:47
  51.3 6.2 %collective-permute-done.2 = bf16[32,7168]{1,0:T(8,128)(2,1)S(1)} collective-permute-done((bf16[32,7168]{1,0:T(8,128)(2,1)S(1)}, bf16[32,7168]{1,0:T(8,128)(2,1)S(1)}, u32[]{:S(2)}, u32[]{:S(2)}) %collective-permute-start.2) | collective-permute-done | bytes 458784 | tf_op jit(solution)/shard_map/ppermute | solution.py:43
  57.4 0.0 collective-permute-start.3
  57.4 0.2 stack_reshape.3
  57.6 0.0 collective-permute-done.5
  57.6 3.0 %collective-permute-start.6 = (bf16[32,7168]{1,0:T(8,128)(2,1)S(1)}, bf16[32,7168]{1,0:T(8,128)(2,1)S(1)}, u32[]{:S(2)}, u32[]{:S(2)}) collective-permute-start(bf16[32,7168]{1,0:T(8,128)(2,1)S(1)} %collective-permute-done.5), channel_id=1, source_target_pairs={{1,0},{2,1},{3,2},{4,3},{5,4},{6,5},{7,6},{0,7},{9,8},{10,9},{11,1... | collective-permute-start | bytes 1376264 | tf_op jit(solution)/shard_map/ppermute | solution.py:47
  60.6 6.0 %collective-permute-done.3 = bf16[32,7168]{1,0:T(8,128)(2,1)} collective-permute-done((bf16[32,7168]{1,0:T(8,128)(2,1)S(1)}, bf16[32,7168]{1,0:T(8,128)(2,1)}, u32[]{:S(2)}, u32[]{:S(2)}) %collective-permute-start.3) | collective-permute-done | bytes 458784 | tf_op jit(solution)/shard_map/ppermute | solution.py:43
  66.6 1.8 %bitcast_dynamic-update-slice_fusion.6 = bf16[8,32,7168]{2,1,0:T(8,128)(2,1)} fusion(bf16[32,7168]{1,0:T(8,128)(2,1)} %collective-permute-done.3), kind=kLoop, calls=%fused_computation.21 | loop fusion | bytes 917504
  68.5 0.8 bitcast_dynamic-update-slice_fusion.5
  69.3 0.8 bitcast_dynamic-update-slice_fusion.4
  70.1 0.8 bitcast_dynamic-update-slice_fusion.3
  70.9 0.8 constant_dynamic-update-slice_fusion
  71.7 0.8 bitcast_dynamic-update-slice_fusion.2
  72.5 0.8 bitcast_dynamic-update-slice_fusion.1
  73.3 0.0 collective-permute-done.6
  73.3 0.8 bitcast_dynamic-update-slice_fusion
  74.1 4.7 %gather_fusion.1 = bf16[8,32,7168]{2,1,0:T(8,128)(2,1)} fusion(bf16[8,32,7168]{2,1,0:T(8,128)(2,1)} %bitcast_dynamic-update-slice_fusion, s32[1024]{0:T(1024)S(1)} %pad_clamp_fusion.1), kind=kCustom, calls=%fused_computation.1 | custom fusion | bytes 7340064 | tf_op jit(solution)/shard_map/gather | solution.py:51
  78.8 4.3 %fusion.3 = f32[256,256]{1,0:T(8,128)S(1)} fusion(bf16[256,7168]{1,0:T(8,128)(2,1)} %bitcast.43, bf16[1,7168,256]{2,1,0:T(8,128)(2,1)} %param.9), kind=kOutput, calls=%fused_computation.9 | convolution fusion | flops 939524096 | bytes 7602176 | tf_op jit(solution)/shard_map/dot_general | solution.py:53
  83.1 10.0 %convolution_convert_fusion = bf16[256,7168]{1,0:T(8,128)(2,1)} fusion(bf16[1,256,7168]{2,1,0:T(8,128)(2,1)} %param.11, bf16[256,7168]{1,0:T(8,128)(2,1)} %bitcast.44, bf16[1,7168,256]{2,1,0:T(8,128)(2,1)} %param.10, f32[256,256]{1,0:T(8,128)S(1)} %fusion.3), kind=kOutput, calls=%fused_computation.5 | convolution fusion | flops 1881276416 | bytes 14942208 | tf_op jit(solution)/shard_map/dot_general | solution.py:57
  93.1 0.0 copy-start.1
  93.1 0.0 reduce-scatter.2.cloned.1.call-update
  93.1 32.1 %reduce-scatter.2.cloned.1.call-done = bf16[32,7168]{1,0:T(8,128)(2,1)} async-done(((bf16[256,7168]{1,0:T(8,128)(2,1)}), bf16[32,7168]{1,0:T(8,128)(2,1)}) %reduce-scatter.2.cloned.1.call-update) | async-done | bytes 458768 | tf_op jit(solution)/shard_map/reduce_scatter | solution.py:56
  125.2 2.0 %reshape.107 = bf16[16,2,7168]{2,1,0:T(2,128)(2,1)} reshape(bf16[32,7168]{1,0:T(8,128)(2,1)} %reduce-scatter.2.cloned.1.call-done) | data formatting | bytes 917504 | tf_op jit(solution)/shard_map/reshape | solution.py:62
  127.2 7.0 %all-to-all-start.1 = ((bf16[16,2,7168]{2,1,0:T(2,128)(2,1)}), bf16[16,2,7168]{2,1,0:T(2,128)(2,1)S(1)}, u32[]{:S(2)}, u32[]{:S(2)}) async-start(bf16[16,2,7168]{2,1,0:T(2,128)(2,1)} %reshape.107), calls=%async_computation.2 | async-start | bytes 917504 | tf_op jit(solution)/shard_map/all_to_all | solution.py:63
  134.2 0.0 copy-done.1
  134.2 0.1 convert_reduce_fusion
  134.3 0.1 convert_divide_fusion
  134.4 9.5 %all-to-all-done.1 = bf16[16,2,7168]{2,1,0:T(2,128)(2,1)S(1)} async-done(((bf16[16,2,7168]{2,1,0:T(2,128)(2,1)}), bf16[16,2,7168]{2,1,0:T(2,128)(2,1)S(1)}, u32[]{:S(2)}, u32[]{:S(2)}) %all-to-all-start.1) | async-done | bytes 458784 | tf_op jit(solution)/shard_map/all_to_all | solution.py:63
  143.9 0.2 reshape.108
  144.1 0.7 gather_fusion.2
  144.8 0.9 fusion.13
  (9 shorter events, 0.1 us)
Async XLA Ops:
  6.5 2.5 %copy-start = (bf16[2,7168]{1,0:T(2,128)(2,1)S(1)}, bf16[2,7168]{1,0:T(2,128)(2,1)}, u32[]{:S(2)}) copy-start(bf16[2,7168]{1,0:T(2,128)(2,1)} %param.6) | copy-start | bytes 86020
  6.5 118.7 %reduce-scatter.2.cloned.1.call-start = ((), (), s32[]{:S(2)}) async-start(), calls=%async_computation.3 | async-start | bytes 4128768 | tf_op jit(solution)/shard_map/reduce_scatter | solution.py:56
  30.1 9.1 %collective-permute-start = (bf16[32,7168]{1,0:T(8,128)(2,1)S(1)}, bf16[32,7168]{1,0:T(8,128)(2,1)S(1)}, u32[]{:S(2)}, u32[]{:S(2)}) collective-permute-start(bf16[32,7168]{1,0:T(8,128)(2,1)S(1)} %reshape.105), channel_id=1, source_target_pairs={{0,1},{1,2},{2,3},{3,4},{4,5},{5,6},{6,7},{7,0},{8,9},{9,10},{10,1... | collective-permute-start | bytes 1376264 | tf_op jit(solution)/shard_map/ppermute | solution.py:43
  39.2 9.1 %collective-permute-start.1 = (bf16[32,7168]{1,0:T(8,128)(2,1)S(1)}, bf16[32,7168]{1,0:T(8,128)(2,1)S(1)}, u32[]{:S(2)}, u32[]{:S(2)}) collective-permute-start(bf16[32,7168]{1,0:T(8,128)(2,1)S(1)} %collective-permute-done), channel_id=1, source_target_pairs={{0,1},{1,2},{2,3},{3,4},{4,5},{5,6},{6,7},{7,0},{8,9},{9,10},{10,1... | collective-permute-start | bytes 1376264 | tf_op jit(solution)/shard_map/ppermute | solution.py:43
  39.2 9.1 %collective-permute-start.4 = (bf16[32,7168]{1,0:T(8,128)(2,1)S(1)}, bf16[32,7168]{1,0:T(8,128)(2,1)S(1)}, u32[]{:S(2)}, u32[]{:S(2)}) collective-permute-start(bf16[32,7168]{1,0:T(8,128)(2,1)S(1)} %reshape.105), channel_id=1, source_target_pairs={{1,0},{2,1},{3,2},{4,3},{5,4},{6,5},{7,6},{0,7},{9,8},{10,9},{11,1... | collective-permute-start | bytes 1376264 | tf_op jit(solution)/shard_map/ppermute | solution.py:47
  48.3 9.1 %collective-permute-start.2 = (bf16[32,7168]{1,0:T(8,128)(2,1)S(1)}, bf16[32,7168]{1,0:T(8,128)(2,1)S(1)}, u32[]{:S(2)}, u32[]{:S(2)}) collective-permute-start(bf16[32,7168]{1,0:T(8,128)(2,1)S(1)} %collective-permute-done.1), channel_id=1, source_target_pairs={{0,1},{1,2},{2,3},{3,4},{4,5},{5,6},{6,7},{7,0},{8,9},{9,10},{10,1... | collective-permute-start | bytes 1376264 | tf_op jit(solution)/shard_map/ppermute | solution.py:43
  48.3 9.3 %collective-permute-start.5 = (bf16[32,7168]{1,0:T(8,128)(2,1)S(1)}, bf16[32,7168]{1,0:T(8,128)(2,1)S(1)}, u32[]{:S(2)}, u32[]{:S(2)}) collective-permute-start(bf16[32,7168]{1,0:T(8,128)(2,1)S(1)} %collective-permute-done.4), channel_id=1, source_target_pairs={{1,0},{2,1},{3,2},{4,3},{5,4},{6,5},{7,6},{0,7},{9,8},{10,9},{11,1... | collective-permute-start | bytes 1376264 | tf_op jit(solution)/shard_map/ppermute | solution.py:47
  57.4 9.2 %collective-permute-start.3 = (bf16[32,7168]{1,0:T(8,128)(2,1)S(1)}, bf16[32,7168]{1,0:T(8,128)(2,1)}, u32[]{:S(2)}, u32[]{:S(2)}) collective-permute-start(bf16[32,7168]{1,0:T(8,128)(2,1)S(1)} %collective-permute-done.2), channel_id=1, source_target_pairs={{0,1},{1,2},{2,3},{3,4},{4,5},{5,6},{6,7},{7,0},{8,9},{9,10},{10,1... | collective-permute-start | bytes 1376264 | tf_op jit(solution)/shard_map/ppermute | solution.py:43
  57.6 15.7 %collective-permute-start.6 = (bf16[32,7168]{1,0:T(8,128)(2,1)S(1)}, bf16[32,7168]{1,0:T(8,128)(2,1)S(1)}, u32[]{:S(2)}, u32[]{:S(2)}) collective-permute-start(bf16[32,7168]{1,0:T(8,128)(2,1)S(1)} %collective-permute-done.5), channel_id=1, source_target_pairs={{1,0},{2,1},{3,2},{4,3},{5,4},{6,5},{7,6},{0,7},{9,8},{10,9},{11,1... | collective-permute-start | bytes 1376264 | tf_op jit(solution)/shard_map/ppermute | solution.py:47
  93.1 41.1 %copy-start.1 = (s32[2,8]{1,0:T(2,128)S(1)}, s32[2,8]{1,0:T(2,128)}, u32[]{:S(2)}) copy-start(s32[2,8]{1,0:T(2,128)} %param.8) | copy-start | bytes 196
  127.2 16.7 %all-to-all-start.1 = ((bf16[16,2,7168]{2,1,0:T(2,128)(2,1)}), bf16[16,2,7168]{2,1,0:T(2,128)(2,1)S(1)}, u32[]{:S(2)}, u32[]{:S(2)}) async-start(bf16[16,2,7168]{2,1,0:T(2,128)(2,1)} %reshape.107), calls=%async_computation.2 | async-start | bytes 917504 | tf_op jit(solution)/shard_map/all_to_all | solution.py:63
Sparse Core Ops, SparseCore 0:
  93.2 31.9 reduce-scatter.1
